TPU v7x, 32 devices: a whole 2x2x4 slice. The times are simulated.
32 devices in a mesh: dp: 16 (over z, y, core), tensor: 2 (over x).
Axes of the slice: x: 2, y: 2, z: 4, core: 2. Of those that a mesh axis runs over, the one named last changes fastest.
Arguments:
- expert_act: bfloat16 [16384, 2880], P(('dp', 'tensor')), may hold values from -6 to 6
- grad_out: bfloat16 [32768, 1440], P(('dp', 'tensor')), may hold values from -6 to 6
- slot_token: int32 [16384], P(('dp', 'tensor')), may hold values from 0 to 1023, as said below
- slot_prob: float32 [16384], P(('dp', 'tensor')), may hold values from 0.2 to 1
- live_count: int32 [32], P(('dp', 'tensor')), may hold values from 128 to 512, as said below
Outputs:
- weight_grad: float32 [2880, 1440], P('dp', 'tensor')
Inputs may be any that keep to these rules, and one draw needn't show every extreme that they name: `slot_token`: each device's 512 entries are distinct token indices of that device. `live_count`: each entry is 512 // j for some j of 1 to 4.
All inputs are finite; a program needn't handle non-finite values.
Results may differ from a plain program's by a relative error of at most 0.0029.
Values may be sent and summed in bfloat16 or wider, within the bound.
No kernel may reach another device: no remote copies, remote signals or barrier semaphores. Data moves between devices by JAX's collectives and lax.ppermute only.
A program may use at most 128 MiB of HBM per device.

v0:
```python
import math

import jax
import jax.numpy as jnp
from jax import lax
from jax.sharding import PartitionSpec as P


def contract(left, right):
    return lax.dot_general(
        left, right, (((0,), (0,)), ((), ())), preferred_element_type=jnp.float32
    )


def shards(expert_act, grad_out, slot_token, slot_prob, live_count):
    slot_count = expert_act.shape[0]
    devices = lax.axis_size("dp") * lax.axis_size("tensor")
    scaling = 1.0 / math.sqrt(slot_count * devices)
    position = jnp.arange(slot_count, dtype=jnp.int32)
    live_mask = position < live_count[0]
    weighting = jnp.where(live_mask, slot_prob, jnp.zeros_like(slot_prob))
    picked = jnp.take(grad_out, slot_token, axis=0).astype(jnp.float32)
    weighted = (picked * weighting[:, None]).astype(jnp.bfloat16)
    both_acts = lax.all_gather(expert_act, "tensor", axis=0, tiled=True)
    both_grads = lax.all_to_all(weighted, "tensor", split_axis=1, concat_axis=0, tiled=True)
    gradient = lax.psum_scatter(
        contract(both_acts, both_grads), "dp", scatter_dimension=0, tiled=True
    )
    return gradient * scaling


def solution(mesh):
    return jax.shard_map(
        shards,
        mesh=mesh,
        in_specs=(
            P(("dp", "tensor"), None),
            P(("dp", "tensor"), None),
            P(("dp", "tensor")),
            P(("dp", "tensor")),
            P(("dp", "tensor")),
        ),
        out_specs=P("dp", "tensor"),
        check_vma=False,
    )
```

profile of v0, /device:TPU:0, one launch (start us, length us, event | category | flops | bytes accessed | tf_op | source)
XLA Modules:
  0.0 293.3 jit_solution(11381292390871192183)
XLA Ops:
  6.5 0.0 all-gather.2.cloned.1.call-start
  6.5 0.7 all-gather.2.cloned.1.call-update
  7.3 0.0 copy-start
  7.3 0.0 all-reduce.3.cloned.1.call-start
  7.3 3.1 %copy.16 = bf16[1024,1440]{1,0:T(8,128)(2,1)S(1)} copy(bf16[1024,1440]{0,1:T(8,128)(2,1)} %param.6) | data formatting | bytes 5898240 | tf_op args[1]
  10.5 0.0 copy-done
  10.5 3.0 %gather_fusion = bf16[512,1440]{1,0:T(8,128)(2,1)} fusion(bf16[1024,1440]{1,0:T(8,128)(2,1)S(1)} %copy.16, s32[1024]{0:T(1024)S(1)} %pad_clamp_fusion), kind=kCustom, calls=%fused_computation | custom fusion | bytes 2951168 | tf_op jit(solution)/shard_map/jit(_take)/gather | solution.py:22
  13.5 0.0 copy-start.1
  13.5 1.7 copy.17
  15.8 0.0 copy-done.1
  15.9 0.4 multiply_convert_fusion
  16.3 37.9 %all_to_all.16 = bf16[512,2,720]{0,2,1:T(8,128)(2,1)S(1)} all-to-all(bf16[512,2,720]{0,2,1:T(8,128)(2,1)S(1)} %multiply_convert_fusion), channel_id=1, replica_groups=mesh['dp'=16,'tensor'=2] {'tensor'}, dimensions={1} | all-to-all | bytes 2949120 | tf_op jit(solution)/shard_map/all_to_all | solution.py:25
  54.1 0.2 copy.22
  54.3 47.6 %all-gather.2.cloned.1.call-done = bf16[1024,2880]{0,1:T(8,128)(2,1)} async-done(((bf16[512,2880]{0,1:T(8,128)(2,1)}), bf16[1024,2880]{0,1:T(8,128)(2,1)}) %all-gather.2.cloned.1.call-update) | async-done | bytes 5898256 | tf_op jit(solution)/shard_map/all_gather | solution.py:24
  101.9 9.6 %convolution_bitcast_fusion = f32[2880,720]{0,1:T(8,128)} fusion(bf16[1024,720]{0,1:T(8,128)(2,1)S(1)} %bitcast.15, bf16[1024,2880]{0,1:T(8,128)(2,1)} %all-gather.2.cloned.1.call-done), kind=kOutput, calls=%fused_computation.1 | convolution fusion | flops 4246732800 | bytes 15667200 | tf_op jit(solution)/shard_map/dot_general | solution.py:10
  111.5 0.0 copy-start.2
  111.5 0.0 all-reduce.3.cloned.1.call-update
  111.6 0.6 copy-done.2
  112.2 0.6 dynamic-slice
  113.4 170.4 %all-reduce.3.cloned.1.call-done = f32[2880,720]{0,1:T(8,128)} async-done(((f32[2880,720]{0,1:T(8,128)}), f32[2880,720]{0,1:T(8,128)}) %all-reduce.3.cloned.1.call-update) | async-done | bytes 8294416
  283.8 1.5 constant_dynamic-slice_fusion
  285.3 0.2 copy.19
  285.6 0.8 broadcast_multiply_fusion
  (4 shorter events, 0.0 us)
Async XLA Ops:
  6.5 95.4 %all-gather.2.cloned.1.call-start = ((), (), s32[]{:S(2)}) async-start(), calls=%async_computation.1 | async-start | bytes 8847360 | tf_op jit(solution)/shard_map/all_gather | solution.py:24
  7.3 3.2 %copy-start = (s32[512]{0:T(512)S(1)}, s32[512]{0:T(512)}, u32[]{:S(2)}) copy-start(s32[512]{0:T(512)} %param.7) | copy-start | bytes 6148
  7.3 276.6 %all-reduce.3.cloned.1.call-start = ((), (), s32[]{:S(2)}) async-start(), calls=%async_computation.2 | async-start | bytes 16957440
  13.5 2.4 copy-start.1
  111.5 0.7 copy-start.2
Sparse Core Ops, SparseCore 0:
  8.9 92.9 all-gather.1
  111.7 172.1 all-reduce.2
where the time goes:
time: 294 us; the launch traced here: 293 us
  waiting for transfers between devices  219 us (74%)
  blocking collectives  37.9 us (13%)
  between operations  14.8 us (5%)
  local copies, waits for them, and re-layouts  10.9 us (4%)
  matrix products  9.63 us (3%)
    unnamed x3, waiting for transfers between devices  171 us
    all_gather x1, waiting for transfers between devices, shards(): both_acts = lax.all_gather(expert_act, 'tensor', axis=0, tiled=True)  47.6 us
    all_to_all x1, blocking collectives, shards(): lax.all_to_all(weighted, 'tensor', split_axis=1, concat_axis=0, tiled=True)  37.9 us
    dot_general x1, matrix products, contract(): lax.dot_general(left, right, (((0,), (0,)), ((), ())), preferred_element_...  9.63 us
  transfers between devices with their start and end apart: 2, of which 2 were waited for; matrix products, arithmetic and copies ran while one was open for 3% of the time, Pallas kernels for 0%

commit v1 on v0

--- a/solution.py
+++ b/solution.py
@@ -1,9 +1,28 @@
+import functools
+import itertools
+import itertools
+import itertools
+import itertools
+import itertools
+import itertools
+import itertools
 import math
 
 import jax
 import jax.numpy as jnp
 from jax import lax
+from jax.experimental import pallas as pl
+from jax.experimental.pallas import tpu as pltpu
 from jax.sharding import PartitionSpec as P
+
+
+CHIP_BITS = "YNF"
+ROUTES = (('YXNF', 10), ('XNFY', 8), ('NXYF', 5))
+SPLIT = frozenset(((0, 0), (0, 1), (0, 2), (1, 0), (1, 1), (1, 2), (2, 0), (2, 1), (2, 2)))
+ORDER = ((1, 0, 1), (1, 0, 0), (0, 0, 1), (2, 0, 1), (1, 1, 1), (2, 0, 0), (1, 1, 0), (0, 0, 0), (2, 1, 1), (0, 1, 1), (2, 1, 0), (0, 1, 0), (1, 2, 1), (1, 2, 0), (2, 2, 1), (2, 2, 0), (0, 2, 1), (0, 2, 0), (2, 3, None), (0, 3, None), (1, 3, None))
+TILE = 256
+GRANT = 24 * 1024 * 1024
+WEIGH_GRANT = 50 * 1024 * 1024
 
 
 def contract(left, right):
@@ -12,7 +31,7 @@
     )
 
 
-def shards(expert_act, grad_out, slot_token, slot_prob, live_count):
+def plain(expert_act, grad_out, slot_token, slot_prob, live_count):
     slot_count = expert_act.shape[0]
     devices = lax.axis_size("dp") * lax.axis_size("tensor")
     scaling = 1.0 / math.sqrt(slot_count * devices)
@@ -29,7 +48,273 @@
     return gradient * scaling
 
 
+def weigh_kernel(grad, token, prob, live, out1, out0, rows, onehot, sems):
+    tokens, slots = onehot.shape
+    count, tile, _ = rows.shape
+    steps, wide = count // 2, out1.shape[0]
+    half = steps * tile
+    x = lax.axis_index("tensor")
+    copies = []
+    for i in range(count):
+        side, t = 1 - i // steps, i % steps
+        start = pl.multiple_of(half * (x ^ side) + t * tile, 8)
+        copy = pltpu.make_async_copy(grad.at[pl.ds(start, tile), :], rows.at[i], sems.at[i])
+        copy.start()
+        copies.append(copy)
+    wanted = jnp.broadcast_to(token[...], (128, slots))
+    for t in range(0, tokens, 128):
+        here = lax.broadcasted_iota(jnp.int32, (128, slots), 0) + t
+        onehot[t : t + 128, :] = jnp.where(here == wanted, 1.0, 0.0).astype(jnp.bfloat16)
+    position = lax.broadcasted_iota(jnp.int32, (1, slots), 1)
+    weight = jnp.where(position < live[0], prob[...], 0.0)
+    for i in range(count):
+        out, t = (out1, out0)[i // steps], i % steps
+        copies[i].wait()
+        picked = jnp.dot(rows[i], onehot[...], preferred_element_type=jnp.float32)
+        out[t * tile : (t + 1) * tile, :] = (picked * weight).astype(jnp.bfloat16)
+    if wide > half:
+        for out in (out1, out0):
+            out[half:, :] = jnp.zeros((wide - half, slots), jnp.bfloat16)
+
+
+def weigh(grad, token, prob, live):
+    width, tokens = grad.shape
+    slots = token.shape[1]
+    half = width // 2
+    wide = -(-half // TILE) * TILE
+    tile = next(t for t in range(min(half, 360), 0, -1) if half % t == 0 and t % 8 == 0)
+    vmem = pl.BlockSpec(memory_space=pltpu.VMEM)
+    hbm = pl.BlockSpec(memory_space=pltpu.HBM)
+    line = pl.BlockSpec((1, slots), lambda i: (0, 0))
+    return pl.pallas_call(
+        weigh_kernel,
+        grid=(1,),
+        out_shape=[jax.ShapeDtypeStruct((wide, slots), jnp.bfloat16)] * 2,
+        in_specs=[hbm, line, line, pl.BlockSpec(memory_space=pltpu.SMEM)],
+        out_specs=[vmem] * 2,
+        scratch_shapes=[
+            pltpu.VMEM((width // tile, tile, tokens), jnp.bfloat16),
+            pltpu.VMEM((tokens, slots), jnp.bfloat16),
+            pltpu.SemaphoreType.DMA((width // tile,)),
+        ],
+        cost_estimate=pl.CostEstimate(
+            flops=2 * width * tokens * slots, bytes_accessed=2 * width * tokens, transcendentals=0
+        ),
+        compiler_params=pltpu.CompilerParams(vmem_limit_bytes=WEIGH_GRANT),
+        name="weigh",
+    )(grad, token, prob, live)
+
+
+def product_kernel(jobs, block, slab, n_out, acts_own, acts_other, *rest):
+    sides = sorted(jobs, reverse=True)
+    w = {a: rest[2 * i : 2 * i + 2] for i, a in enumerate(sides)}
+    rest = rest[2 * len(sides) :]
+    outs, (left,) = rest[:n_out], rest[n_out:]
+    chip = lax.axis_index("dp") // 2
+    core = lax.axis_index("dp") % 2
+    wide, slots = w[sides[0]][0].shape
+    base = 0
+    for a in sides:
+        at = base
+        for q, row, n, _, _ in jobs[a]:
+            start = pl.multiple_of(block * (chip ^ q) + (block - slab) * core + row, 8)
+            left[at : at + n, :slots] = acts_own[pl.ds(start, n), :]
+            left[at : at + n, slots:] = acts_other[pl.ds(start, n), :]
+            at += n
+        rows = at - base
+
+        @pl.loop(0, wide, step=TILE)
+        def _(t):
+            t = pl.multiple_of(t, TILE)
+            total = None
+            for s, right in enumerate(w[a]):
+                term = lax.dot_general(
+                    left[base : base + rows, s * slots : (s + 1) * slots],
+                    right[pl.ds(t, TILE), :],
+                    (((1,), (1,)), ((), ())),
+                    preferred_element_type=jnp.float32,
+                )
+                total = term if total is None else total + term
+            at = 0
+            for _, _, n, out, index in jobs[a]:
+                outs[out][index + (slice(None), pl.ds(t, TILE))] = total[at : at + n].astype(
+                    outs[out].dtype
+                )
+                at += n
+
+        base += rows
+
+
+def product(jobs, shapes, block, slab, acts_own, acts_other, w):
+    rows = sum(job[2] for a in jobs for job in jobs[a])
+    wide, slots = w[0][0].shape
+    weights = [value for a in sorted(jobs, reverse=True) for value in w[a]]
+    vmem = pl.BlockSpec(memory_space=pltpu.VMEM)
+    return pl.pallas_call(
+        functools.partial(product_kernel, jobs, block, slab, len(shapes)),
+        out_shape=[jax.ShapeDtypeStruct(s, t) for s, t in shapes],
+        in_specs=[vmem] * (2 + len(weights)),
+        out_specs=[vmem] * len(shapes),
+        scratch_shapes=[pltpu.VMEM((rows, 2 * slots), jnp.bfloat16)],
+        cost_estimate=pl.CostEstimate(
+            flops=4 * rows * wide * slots,
+            bytes_accessed=4 * (rows + 2 * wide) * slots,
+            transcendentals=0,
+        ),
+        compiler_params=pltpu.CompilerParams(vmem_limit_bytes=GRANT),
+    )(acts_own, acts_other, *weights)
+
+
+def finish_kernel(groups, skip, scaling, *refs):
+    ins, out = refs[:-1], refs[-1]
+    rows, half = out.shape
+    core = lax.axis_index("dp") % 2
+    parts, at = [], 0
+    for count in groups:
+        total = None
+        for ref in ins[at : at + count]:
+            value = ref[(0,) * (len(ref.shape) - 2)].astype(jnp.float32)
+            total = value if total is None else total + value
+        parts.append(total[:, :half])
+        at += count
+    whole = jnp.concatenate(parts, axis=0)
+    picked = jnp.where(core == 0, whole[:rows], whole[skip : skip + rows])
+    out[...] = picked * scaling
+
+
+def finish(groups, rows, half, skip, scaling, terms):
+    vmem = pl.BlockSpec(memory_space=pltpu.VMEM)
+    return pl.pallas_call(
+        functools.partial(finish_kernel, groups, skip, scaling),
+        out_shape=jax.ShapeDtypeStruct((rows, half), jnp.float32),
+        in_specs=[vmem] * len(terms),
+        out_specs=vmem,
+        compiler_params=pltpu.CompilerParams(vmem_limit_bytes=GRANT),
+        name="finish",
+    )(*terms)
+
+
+def shares(slab):
+    groups, total = slab // 8, sum(share for _, share in ROUTES)
+    marks, seen = [0], 0
+    for _, share in ROUTES:
+        seen += share
+        marks.append(8 * round(groups * seen / total))
+    return marks
+
+
+def plan_of(r, i):
+    return f"part_{r}_{i}" if i < 2 else "part_rest"
+
+
+def staged(expert_act, grad_out, slot_token, slot_prob, live_count):
+    dp, tp = lax.axis_size("dp"), lax.axis_size("tensor")
+    slot_count, wide = expert_act.shape
+    half = grad_out.shape[1] // 2
+    lanes = -(-half // TILE) * TILE
+    scaling = 1.0 / math.sqrt(slot_count * dp * tp)
+    block = wide // (dp // 2)
+    rows = block // 2
+    slab = -(-rows // 8) * 8
+    f32, bf16 = jnp.float32, jnp.bfloat16
+    depth = len(ROUTES[0][0])
+
+    def send(value, step):
+        if step == "X":
+            return lax.ppermute(value, "tensor", [(0, 1), (1, 0)])
+        flip = 1 if step == "core" else 2 << CHIP_BITS.index(step)
+        return lax.ppermute(value, "dp", [(i, i ^ flip) for i in range(dp)])
+
+    def owner(route, bits):
+        a, q = 0, 0
+        for step, bit in zip(route, bits):
+            if step == "X":
+                a = bit
+            else:
+                q |= bit << CHIP_BITS.index(step)
+        return a, q
+
+    acts = expert_act.T
+    other_acts = send(acts, "core")
+    routed = grad_out.T, slot_token[None], slot_prob[None], live_count
+    w1, w0 = weigh(*routed)
+    other_w1 = send(w1, "core")
+    other_w0 = send(w0, "core")
+    w = (w0, other_w0), (w1, other_w1)
+
+    marks = shares(slab)
+    plans = {}
+
+    def want(plan, key, dtype, route, head, row, n):
+        jobs, shapes, keys = plans.setdefault(plan, ({}, [], []))
+        free = depth - len(head)
+        for index in itertools.product(range(2), repeat=free):
+            a, q = owner(route, head + index)
+            jobs.setdefault(a, []).append((q, row, n, len(shapes), index))
+        shapes.append(((2,) * free + (n, lanes), dtype))
+        keys.append(key)
+
+    for r, (route, _) in enumerate(ROUTES):
+        row, n = marks[r], marks[r + 1] - marks[r]
+        for i in range(depth):
+            plan, dtype = plan_of(r, i), f32 if i else bf16
+            head = (0,) * i + (1,)
+            if (r, i) in SPLIT:
+                want(plan, (r, i, 1), dtype, route, head + (1,), row, n)
+                want(plan, (r, i, 0), dtype, route, head + (0,), row, n)
+            else:
+                want(plan, (r, i, None), dtype, route, head, row, n)
+        want(plan_of(r, depth), (r, depth), f32, route, (0,) * depth, row, n)
+
+    part = {}
+    for (jobs, shapes, keys) in plans.values():
+        values = product(jobs, shapes, block, slab, acts, other_acts, w)
+        part.update(zip(keys, values))
+
+    got = {}
+
+    def received(r, i, bits):
+        if (r, i) in SPLIT:
+            return got[r, i, bits[0]][tuple(bits[1:])]
+        return got[r, i, None][tuple(bits)]
+
+    def emit(r, i, which):
+        value = part[r, i, which]
+        if i > 0:
+            extra = () if which is None else (which,)
+            for j in range(i):
+                value = value + received(r, j, (0,) * (i - j - 1) + (1,) + extra).astype(f32)
+            value = value.astype(bf16)
+        got[r, i, which] = send(value, ROUTES[r][0][i])
+
+    for r, i, which in ORDER:
+        emit(r, i, which)
+
+    terms, groups = [], []
+    for r in range(len(ROUTES)):
+        terms.append(part[r, depth])
+        for i in range(depth):
+            terms.append(got[r, i, 0 if (r, i) in SPLIT else None])
+        groups.append(depth + 1)
+    return finish(groups, rows, half, slab - rows, scaling, terms)
+
+
 def solution(mesh):
+    dp, tp = mesh.shape["dp"], mesh.shape["tensor"]
+
+    def shards(expert_act, grad_out, slot_token, slot_prob, live_count):
+        wide, width = expert_act.shape[1], grad_out.shape[1]
+        fits = (
+            tp == 2
+            and dp == 2 << len(CHIP_BITS)
+            and wide % (4 * dp) == 0
+            and width % 16 == 0
+            and expert_act.shape[0] % 128 == 0
+            and grad_out.shape[0] % 128 == 0
+        )
+        form = staged if fits else plain
+        return form(expert_act, grad_out, slot_token, slot_prob, live_count)
+
     return jax.shard_map(
         shards,
         mesh=mesh,

time: 294 us -> 81.9 us (0.28)
  waiting for transfers between devices: 219 us -> 30 us
  blocking collectives: 37.9 us -> 0 us
  starting transfers between devices: 0.04 us -> 33.4 us
  Pallas kernels: 0 us -> 15.3 us
  between operations: 14.8 us -> 1.1 us
  matrix products: 9.63 us -> 0 us
  local copies, waits for them, and re-layouts: 10.9 us -> 1.36 us
    unnamed x3 -> x0, waiting for transfers between devices: 171 us -> none
    all_gather x1 -> x0, waiting for transfers between devices: 47.6 us -> none  [shards(): both_acts = lax.all_gather(expert_act, 'tensor', axis=0, tiled=True)]
    all_to_all x1 -> x0, blocking collectives: 37.9 us -> none  [shards(): lax.all_to_all(weighted, 'tensor', split_axis=1, concat_axis=0, tiled=True)]
    ppermute x0 -> x24, starting transfers between devices: none -> 33.4 us  [the longest x18 26.7 us: send(): return lax.ppermute(value, 'dp', [(i, i ^ flip) for i in range(dp)])]
    ppermute x0 -> x24, waiting for transfers between devices: none -> 30 us  [the longest x18 20.9 us: send(): return lax.ppermute(value, 'dp', [(i, i ^ flip) for i in range(dp)])]
    pallas_call x0 -> x9, Pallas kernels: none -> 15.3 us  [the longest x7 10.9 us: product(): pl.pallas_call(functools.partial(product_kernel, jobs, block, slab, len(s...]
    dot_general x1 -> x0, matrix products: 9.63 us -> none  [contract(): lax.dot_general(left, right, (((0,), (0,)), ((), ())), preferred_element_...]
    gather x2 -> x0, local copies, waits for them, and re-layouts: 4.67 us -> none  [shards(): picked = jnp.take(grad_out, slot_token, axis=0).astype(jnp.float32)]
  transfers between devices with their start and end apart: 2 -> 24, of which waited for: 2 -> 9; matrix products, arithmetic and copies ran while one was open for 3% -> 1% of each run, Pallas kernels for 0% -> 15%
where the time goes in v1:
time: 81.9 us; the launch traced here: 81.7 us
  starting transfers between devices  33.4 us (41%)
  waiting for transfers between devices  30 us (37%)
  Pallas kernels  15.3 us (19%)
  local copies, waits for them, and re-layouts  1.36 us (2%)
  between operations  1.1 us (1%)
    ppermute x18, starting transfers between devices, send(): return lax.ppermute(value, 'dp', [(i, i ^ flip) for i in range(dp)])  26.7 us
    ppermute x18, waiting for transfers between devices, send(): return lax.ppermute(value, 'dp', [(i, i ^ flip) for i in range(dp)])  20.9 us
    pallas_call x7, Pallas kernels, product(): pl.pallas_call(functools.partial(product_kernel, jobs, block, slab, len(s...  10.9 us
    ppermute x6, waiting for transfers between devices, send(): return lax.ppermute(value, 'tensor', [(0, 1), (1, 0)])  9.12 us
    ppermute x6, starting transfers between devices, send(): return lax.ppermute(value, 'tensor', [(0, 1), (1, 0)])  6.68 us
    pallas_call x1, Pallas kernels, weigh(): pl.pallas_call(weigh_kernel, grid=(1,), out_shape=[jax.ShapeDtypeStruct((...  3.36 us
  transfers between devices with their start and end apart: 24, of which 9 were waited for; matrix products, arithmetic and copies ran while one was open for 1% of the time, Pallas kernels for 15%

profile of v1, /device:TPU:0, one launch (start us, length us, event | category | flops | bytes accessed | tf_op | source)
XLA Modules:
  0.0 81.7 jit_solution(11621145744166421322)
XLA Ops:
  0.0 0.5 collective-permute-start
  1.4 0.7 copy-done.1
  2.1 0.7 copy-done.2
  2.8 3.4 %weigh.1 = (bf16[768,512]{1,0:T(8,128)(2,1)S(1)}, bf16[768,512]{1,0:T(8,128)(2,1)S(1)}) custom-call(bf16[1440,1024]{1,0:T(8,128)(2,1)} %bitcast.134, s32[1,512]{1,0:T(1,128)S(1)} %bitcast.132, f32[1,512]{1,0:T(1,128)S(1)} %bitcast.133, s32[1]{0:T(128)S(6)} %copy.6.live), custom_call_target="tpu_custom_call" | custom-call | flops 1509949440 | bytes 2949120 | tf_op jit(solution)/shard_map/weigh/pallas_call | solution.py:89
  6.1 0.1 collective-permute-start.1
  6.2 0.5 collective-permute-start.2
  6.7 1.8 %collective-permute-done.1.rest_1_.rest_3_ = bf16[768,512]{1,0:T(8,128)(2,1)S(1)} collective-permute-done((bf16[768,512]{1,0:T(8,128)(2,1)S(1)}, bf16[768,512]{1,0:T(8,128)(2,1)S(1)}, u32[]{:S(2)}, u32[]{:S(2)}) %collective-permute-start.1) | collective-permute-done | bytes 786464 | tf_op jit(solution)/shard_map/ppermute | solution.py:226
  8.5 1.1 %collective-permute-done.2.rest_1_ = bf16[768,512]{1,0:T(8,128)(2,1)S(1)} collective-permute-done((bf16[768,512]{1,0:T(8,128)(2,1)S(1)}, bf16[768,512]{1,0:T(8,128)(2,1)S(1)}, u32[]{:S(2)}, u32[]{:S(2)}) %collective-permute-start.2) | collective-permute-done | bytes 786464 | tf_op jit(solution)/shard_map/ppermute | solution.py:226
  9.6 0.0 collective-permute-done.acts_other
  9.6 2.0 %shard_map.60 = (bf16[2,2,40,768]{3,2,1,0:T(8,128)(2,1)S(1)}, bf16[2,2,40,768]{3,2,1,0:T(8,128)(2,1)S(1)}) custom-call(bf16[2880,512]{1,0:T(8,128)(2,1)S(1)} %bitcast.125, bf16[2880,512]{1,0:T(8,128)(2,1)S(1)} %collective-permute-done.acts_other, bf16[768,512]{1,0:T(8,128)(2,1)S(1)} %get-tuple-element.33.rest_0_, ...), custom_call_target="tpu_custom_call" | custom-call | flops 503316480 | bytes 3801088 | tf_op jit(solution)/shard_map/pallas_call | solution.py:153
  11.6 2.7 %collective-permute-start.17 = (bf16[2,2,40,768]{3,2,1,0:T(8,128)(2,1)S(1)}, bf16[2,2,40,768]{3,2,1,0:T(8,128)(2,1)S(1)}, u32[]{:S(2)}, u32[]{:S(2)}) collective-permute-start(bf16[2,2,40,768]{3,2,1,0:T(8,128)(2,1)S(1)} %get-tuple-element.50), channel_id=1, source_target_pairs={{0,8},{2,10},{4,12},{6,14},{8,0},{10,2},{12,4},{14,6},{16,24},{18,... | collective-permute-start | bytes 737288 | tf_op jit(solution)/shard_map/ppermute | solution.py:226
  14.3 0.1 collective-permute-start.18
  14.4 1.5 %shard_map.58 = (bf16[2,2,64,768]{3,2,1,0:T(8,128)(2,1)S(1)}, bf16[2,2,64,768]{3,2,1,0:T(8,128)(2,1)S(1)}) custom-call(bf16[2880,512]{1,0:T(8,128)(2,1)S(1)} %bitcast.126, bf16[2880,512]{1,0:T(8,128)(2,1)S(1)} %collective-permute-done.acts_other, bf16[768,512]{1,0:T(8,128)(2,1)S(1)} %get-tuple-element.33.rest_0_, ...), custom_call_target="tpu_custom_call" | custom-call | flops 805306368 | bytes 4194304 | tf_op jit(solution)/shard_map/pallas_call | solution.py:153
  15.9 1.9 %collective-permute-start.10 = (bf16[2,2,64,768]{3,2,1,0:T(8,128)(2,1)S(1)}, bf16[2,2,64,768]{3,2,1,0:T(8,128)(2,1)S(1)}, u32[]{:S(2)}, u32[]{:S(2)}) collective-permute-start(bf16[2,2,64,768]{3,2,1,0:T(8,128)(2,1)S(1)} %get-tuple-element.42), channel_id=1, source_target_pairs={{0,1},{1,0},{2,3},{3,2},{4,5},{5,4},{6,7},{7,6},{8,9},{9,8},{10,11... | collective-permute-start | bytes 1179656 | tf_op jit(solution)/shard_map/ppermute | solution.py:224
  17.8 0.2 collective-permute-start.11
  18.0 2.3 %shard_map.56 = (bf16[2,2,80,768]{3,2,1,0:T(8,128)(2,1)S(1)}, bf16[2,2,80,768]{3,2,1,0:T(8,128)(2,1)S(1)}) custom-call(bf16[2880,512]{1,0:T(8,128)(2,1)S(1)} %bitcast.127, bf16[2880,512]{1,0:T(8,128)(2,1)S(1)} %collective-permute-done.acts_other, bf16[768,512]{1,0:T(8,128)(2,1)S(1)} %get-tuple-element.33.rest_0_, ...), custom_call_target="tpu_custom_call" | custom-call | flops 1006632960 | bytes 4456448 | tf_op jit(solution)/shard_map/pallas_call | solution.py:153
  20.3 2.0 %collective-permute-start.3 = (bf16[2,2,80,768]{3,2,1,0:T(8,128)(2,1)S(1)}, bf16[2,2,80,768]{3,2,1,0:T(8,128)(2,1)S(1)}, u32[]{:S(2)}, u32[]{:S(2)}) collective-permute-start(bf16[2,2,80,768]{3,2,1,0:T(8,128)(2,1)S(1)} %get-tuple-element.34), channel_id=1, source_target_pairs={{0,4},{2,6},{4,0},{6,2},{8,12},{10,14},{12,8},{14,10},{16,20},{18,... | collective-permute-start | bytes 1474568 | tf_op jit(solution)/shard_map/ppermute | solution.py:226
  22.2 1.2 %shard_map.57 = (f32[2,80,768]{2,1,0:T(8,128)S(1)}, f32[2,80,768]{2,1,0:T(8,128)S(1)}) custom-call(bf16[2880,512]{1,0:T(8,128)(2,1)S(1)} %bitcast.128, bf16[2880,512]{1,0:T(8,128)(2,1)S(1)} %collective-permute-done.acts_other, bf16[768,512]{1,0:T(8,128)(2,1)S(1)} %get-tuple-element.33.rest_0_, bf16[768,512]{1,0:T(8,128)(2,1)S(1)} %collective-permute-done.2.rest_1_), custom_call_target="tpu_custom_call" | custom-call | flops 503316480 | bytes 3801088 | tf_op jit(solution)/shard_map/pallas_call | solution.py:153
  23.4 1.0 %shard_map.61 = (f32[2,40,768]{2,1,0:T(8,128)S(1)}, f32[2,40,768]{2,1,0:T(8,128)S(1)}) custom-call(bf16[2880,512]{1,0:T(8,128)(2,1)S(1)} %bitcast.129, bf16[2880,512]{1,0:T(8,128)(2,1)S(1)} %collective-permute-done.acts_other, bf16[768,512]{1,0:T(8,128)(2,1)S(1)} %get-tuple-element.33.rest_0_, bf16[768,512]{1,0:T(8,128)(2,1)S(1)} %collective-permute-done.2.rest_1_), custom_call_target="tpu_custom_call" | custom-call | flops 251658240 | bytes 3473408 | tf_op jit(solution)/shard_map/pallas_call | solution.py:153
  24.4 1.1 %shard_map.59 = (f32[2,64,768]{2,1,0:T(8,128)S(1)}, f32[2,64,768]{2,1,0:T(8,128)S(1)}) custom-call(bf16[2880,512]{1,0:T(8,128)(2,1)S(1)} %bitcast.130, bf16[2880,512]{1,0:T(8,128)(2,1)S(1)} %collective-permute-done.acts_other, bf16[768,512]{1,0:T(8,128)(2,1)S(1)} %get-tuple-element.31.rest_0_.rest_2_, bf16[768,512]{1,0:T(8,128)(2,1)S(1)} %collective-permute-done.1.rest_1_.rest_3_), custom_call_target="tpu_custom_call" | custom-call | flops 402653184 | bytes 3670016 | tf_op jit(solution)/shard_map/pallas_call | solution.py:153
  25.5 1.9 %shard_map.55 = (f32[80,768]{1,0:T(8,128)S(1)}, f32[80,768]{1,0:T(8,128)S(1)}, f32[80,768]{1,0:T(8,128)S(1)}, f32[80,768]{1,0:T(8,128)S(1)}, f32[64,768]{1,0:T(8...) custom-call(bf16[2880,512]{1,0:T(8,128)(2,1)S(1)} %bitcast.131, ...), custom_call_target="tpu_custom_call" | custom-call | flops 1157627904 | bytes 4653056 | tf_op jit(solution)/shard_map/pallas_call | solution.py:153
  27.4 0.0 collective-permute-done.18
  27.4 0.4 collective-permute-start.4
  27.8 0.1 fusion.4
  27.8 7.7 %collective-permute-done.11 = bf16[2,2,64,768]{3,2,1,0:T(8,128)(2,1)S(1)} collective-permute-done((bf16[2,2,64,768]{3,2,1,0:T(8,128)(2,1)S(1)}, bf16[2,2,64,768]{3,2,1,0:T(8,128)(2,1)S(1)}, u32[]{:S(2)}, u32[]{:S(2)}) %collective-permute-start.11) | collective-permute-done | bytes 393248 | tf_op jit(solution)/shard_map/ppermute | solution.py:224
  35.5 1.6 %collective-permute-start.20 = (bf16[2,40,768]{2,1,0:T(8,128)(2,1)S(1)}, bf16[2,40,768]{2,1,0:T(8,128)(2,1)S(1)}, u32[]{:S(2)}, u32[]{:S(2)}) collective-permute-start(bf16[2,40,768]{2,1,0:T(8,128)(2,1)S(1)} %get-tuple-element.67), channel_id=1, source_target_pairs={{0,1},{1,0},{2,3},{3,2},{4,5},{5,4},{6,7},{7,6},{8,9},{9,8},{10,11... | collective-permute-start | bytes 368648 | tf_op jit(solution)/shard_map/ppermute | solution.py:224
  37.1 0.1 fusion.2
  37.2 6.4 %collective-permute-done.4 = bf16[2,2,80,768]{3,2,1,0:T(8,128)(2,1)S(1)} collective-permute-done((bf16[2,2,80,768]{3,2,1,0:T(8,128)(2,1)S(1)}, bf16[2,2,80,768]{3,2,1,0:T(8,128)(2,1)S(1)}, u32[]{:S(2)}, u32[]{:S(2)}) %collective-permute-start.4) | collective-permute-done | bytes 491552 | tf_op jit(solution)/shard_map/ppermute | solution.py:226
  43.5 1.6 %collective-permute-start.19 = (bf16[2,40,768]{2,1,0:T(8,128)(2,1)S(1)}, bf16[2,40,768]{2,1,0:T(8,128)(2,1)S(1)}, u32[]{:S(2)}, u32[]{:S(2)}) collective-permute-start(bf16[2,40,768]{2,1,0:T(8,128)(2,1)S(1)} %get-tuple-element.68), channel_id=1, source_target_pairs={{0,1},{1,0},{2,3},{3,2},{4,5},{5,4},{6,7},{7,6},{8,9},{9,8},{10,11... | collective-permute-start | bytes 368648 | tf_op jit(solution)/shard_map/ppermute | solution.py:224
  45.1 0.1 fusion
  45.2 0.0 collective-permute-done.17.refs_11_
  45.2 1.6 %collective-permute-start.13 = (bf16[2,64,768]{2,1,0:T(8,128)(2,1)S(1)}, bf16[2,64,768]{2,1,0:T(8,128)(2,1)S(1)}, u32[]{:S(2)}, u32[]{:S(2)}) collective-permute-start(bf16[2,64,768]{2,1,0:T(8,128)(2,1)S(1)} %get-tuple-element.63), channel_id=1, source_target_pairs={{0,8},{2,10},{4,12},{6,14},{8,0},{10,2},{12,4},{14,6},{16,24},{18,... | collective-permute-start | bytes 589832 | tf_op jit(solution)/shard_map/ppermute | solution.py:226
  46.9 0.0 collective-permute-done.20
  46.9 0.5 collective-permute-start.6
  47.4 0.1 fusion.14
  47.5 0.0 collective-permute-done.10.refs_6_
  47.5 1.6 %collective-permute-start.22 = (bf16[40,768]{1,0:T(8,128)(2,1)S(1)}, bf16[40,768]{1,0:T(8,128)(2,1)S(1)}, u32[]{:S(2)}, u32[]{:S(2)}) collective-permute-start(bf16[40,768]{1,0:T(8,128)(2,1)S(1)} %get-tuple-element.65), channel_id=1, source_target_pairs={{0,4},{2,6},{4,0},{6,2},{8,12},{10,14},{12,8},{14,10},{16,20},{18,... | collective-permute-start | bytes 184328 | tf_op jit(solution)/shard_map/ppermute | solution.py:226
  49.1 2.0 %collective-permute-done.13 = bf16[2,64,768]{2,1,0:T(8,128)(2,1)S(1)} collective-permute-done((bf16[2,64,768]{2,1,0:T(8,128)(2,1)S(1)}, bf16[2,64,768]{2,1,0:T(8,128)(2,1)S(1)}, u32[]{:S(2)}, u32[]{:S(2)}) %collective-permute-start.13) | collective-permute-done | bytes 196640 | tf_op jit(solution)/shard_map/ppermute | solution.py:226
  51.1 1.6 %collective-permute-start.12 = (bf16[2,64,768]{2,1,0:T(8,128)(2,1)S(1)}, bf16[2,64,768]{2,1,0:T(8,128)(2,1)S(1)}, u32[]{:S(2)}, u32[]{:S(2)}) collective-permute-start(bf16[2,64,768]{2,1,0:T(8,128)(2,1)S(1)} %get-tuple-element.64), channel_id=1, source_target_pairs={{0,8},{2,10},{4,12},{6,14},{8,0},{10,2},{12,4},{14,6},{16,24},{18,... | collective-permute-start | bytes 589832 | tf_op jit(solution)/shard_map/ppermute | solution.py:226
  52.7 0.1 fusion.10
  52.8 0.0 collective-permute-done.3.refs_1_
  52.8 0.9 %collective-permute-start.5 = (bf16[2,80,768]{2,1,0:T(8,128)(2,1)S(1)}, bf16[2,80,768]{2,1,0:T(8,128)(2,1)S(1)}, u32[]{:S(2)}, u32[]{:S(2)}) collective-permute-start(bf16[2,80,768]{2,1,0:T(8,128)(2,1)S(1)} %get-tuple-element.62), channel_id=1, source_target_pairs={{0,1},{1,0},{2,3},{3,2},{4,5},{5,4},{6,7},{7,6},{8,9},{9,8},{10,11... | collective-permute-start | bytes 737288 | tf_op jit(solution)/shard_map/ppermute | solution.py:224
  53.7 1.4 %collective-permute-done.6 = bf16[2,80,768]{2,1,0:T(8,128)(2,1)S(1)} collective-permute-done((bf16[2,80,768]{2,1,0:T(8,128)(2,1)S(1)}, bf16[2,80,768]{2,1,0:T(8,128)(2,1)S(1)}, u32[]{:S(2)}, u32[]{:S(2)}) %collective-permute-start.6) | collective-permute-done | bytes 245792 | tf_op jit(solution)/shard_map/ppermute | solution.py:224
  55.1 2.8 %collective-permute-start.15 = (bf16[64,768]{1,0:T(8,128)(2,1)S(1)}, bf16[64,768]{1,0:T(8,128)(2,1)S(1)}, u32[]{:S(2)}, u32[]{:S(2)}) collective-permute-start(bf16[64,768]{1,0:T(8,128)(2,1)S(1)} %get-tuple-element.59), channel_id=1, source_target_pairs={{0,16},{2,18},{4,20},{6,22},{8,24},{10,26},{12,28},{14,30},{16,0},... | collective-permute-start | bytes 294920 | tf_op jit(solution)/shard_map/ppermute | solution.py:226
  57.9 0.1 fusion.6
  58.0 1.6 %collective-permute-start.21 = (bf16[40,768]{1,0:T(8,128)(2,1)S(1)}, bf16[40,768]{1,0:T(8,128)(2,1)S(1)}, u32[]{:S(2)}, u32[]{:S(2)}) collective-permute-start(bf16[40,768]{1,0:T(8,128)(2,1)S(1)} %get-tuple-element.66), channel_id=1, source_target_pairs={{0,4},{2,6},{4,0},{6,2},{8,12},{10,14},{12,8},{14,10},{16,20},{18,... | collective-permute-start | bytes 184328 | tf_op jit(solution)/shard_map/ppermute | solution.py:226
  59.5 2.9 %collective-permute-done.15 = bf16[64,768]{1,0:T(8,128)(2,1)S(1)} collective-permute-done((bf16[64,768]{1,0:T(8,128)(2,1)S(1)}, bf16[64,768]{1,0:T(8,128)(2,1)S(1)}, u32[]{:S(2)}, u32[]{:S(2)}) %collective-permute-start.15) | collective-permute-done | bytes 98336 | tf_op jit(solution)/shard_map/ppermute | solution.py:226
  62.4 0.0 collective-permute-start.8
  62.4 0.1 fusion.12
  62.5 0.0 collective-permute-done.5.refs_2_
  62.5 3.9 %collective-permute-start.14 = (bf16[64,768]{1,0:T(8,128)(2,1)S(1)}, bf16[64,768]{1,0:T(8,128)(2,1)S(1)}, u32[]{:S(2)}, u32[]{:S(2)}) collective-permute-start(bf16[64,768]{1,0:T(8,128)(2,1)S(1)} %get-tuple-element.60), channel_id=1, source_target_pairs={{0,16},{2,18},{4,20},{6,22},{8,24},{10,26},{12,28},{14,30},{16,0},... | collective-permute-start | bytes 294920 | tf_op jit(solution)/shard_map/ppermute | solution.py:226
  66.4 1.3 %collective-permute-done.8 = bf16[80,768]{1,0:T(8,128)(2,1)S(1)} collective-permute-done((bf16[80,768]{1,0:T(8,128)(2,1)S(1)}, bf16[80,768]{1,0:T(8,128)(2,1)S(1)}, u32[]{:S(2)}, u32[]{:S(2)}) %collective-permute-start.8) | collective-permute-done | bytes 122912 | tf_op jit(solution)/shard_map/ppermute | solution.py:226
  67.6 4.3 %collective-permute-start.16 = (bf16[64,768]{1,0:T(8,128)(2,1)S(1)}, bf16[64,768]{1,0:T(8,128)(2,1)S(1)}, u32[]{:S(2)}, u32[]{:S(2)}) collective-permute-start(bf16[64,768]{1,0:T(8,128)(2,1)S(1)} %fusion.12), channel_id=1, source_target_pairs={{0,4},{2,6},{4,0},{6,2},{8,12},{10,14},{12,8},{14,10},{16,20},{18,... | collective-permute-start | bytes 294920 | tf_op jit(solution)/shard_map/ppermute | solution.py:226
  72.0 0.1 fusion.8
  72.0 0.0 collective-permute-done.19.refs_12_
  72.0 0.1 collective-permute-start.7
  72.1 2.0 %collective-permute-start.9 = (bf16[80,768]{1,0:T(8,128)(2,1)S(1)}, bf16[80,768]{1,0:T(8,128)(2,1)S(1)}, u32[]{:S(2)}, u32[]{:S(2)}) collective-permute-start(bf16[80,768]{1,0:T(8,128)(2,1)S(1)} %fusion.8), channel_id=1, source_target_pairs={{0,16},{2,18},{4,20},{6,22},{8,24},{10,26},{12,28},{14,30},{16,0},... | collective-permute-start | bytes 368648 | tf_op jit(solution)/shard_map/ppermute | solution.py:226
  74.1 0.0 collective-permute-done.21.refs_13_
  74.1 1.1 %collective-permute-start.23 = (bf16[40,768]{1,0:T(8,128)(2,1)S(1)}, bf16[40,768]{1,0:T(8,128)(2,1)S(1)}, u32[]{:S(2)}, u32[]{:S(2)}) collective-permute-start(bf16[40,768]{1,0:T(8,128)(2,1)S(1)} %fusion.16), channel_id=1, source_target_pairs={{0,16},{2,18},{4,20},{6,22},{8,24},{10,26},{12,28},{14,30},{16,0},... | collective-permute-start | bytes 184328 | tf_op jit(solution)/shard_map/ppermute | solution.py:226
  75.2 5.4 %collective-permute-done.23.refs_14_ = bf16[40,768]{1,0:T(8,128)(2,1)S(1)} collective-permute-done((bf16[40,768]{1,0:T(8,128)(2,1)S(1)}, bf16[40,768]{1,0:T(8,128)(2,1)S(1)}, u32[]{:S(2)}, u32[]{:S(2)}) %collective-permute-start.23) | collective-permute-done | bytes 61472 | tf_op jit(solution)/shard_map/ppermute | solution.py:226
  80.6 0.0 collective-permute-done.14.refs_8_
  80.7 0.0 collective-permute-done.16.refs_9_
  80.7 0.0 collective-permute-done.7.refs_3_
  80.7 1.0 %finish.1 = f32[180,720]{1,0:T(8,128)} custom-call(f32[80,768]{1,0:T(8,128)S(1)} %get-tuple-element.32.refs_0_, bf16[2,2,80,768]{3,2,1,0:T(8,128)(2,1)S(1)} %collective-permute-done.3.refs_1_, bf16[2,80,768]{2,1,0:T(8,128)(2,1)S(1)} %collective-permute-done.5.refs_2_, bf16[80,768]{1,0:T(8,128)(2,1)S(1)} %collective-permute-done.7.refs_3_, ...), custom_call_target="tpu_custom_call" | custom-call | tf_op jit(solution)/shard_map/finish/pallas_call | solution.py:187
  (8 shorter events, 0.1 us)
Async XLA Ops:
  0.0 9.6 %copy-start = (bf16[512,2880]{0,1:T(8,128)(2,1)S(1)}, bf16[512,2880]{0,1:T(8,128)(2,1)}, u32[]{:S(2)}) copy-start(bf16[512,2880]{0,1:T(8,128)(2,1)} %param.5) | copy-start | bytes 8847364
  0.0 9.6 %collective-permute-start = (bf16[2880,512]{1,0:T(8,128)(2,1)}, bf16[2880,512]{1,0:T(8,128)(2,1)S(1)}, u32[]{:S(2)}, u32[]{:S(2)}) collective-permute-start(bf16[2880,512]{1,0:T(8,128)(2,1)} %bitcast.124), channel_id=1, source_target_pairs={{0,2},{2,0},{4,6},{6,4},{8,10},{10,8},{12,14},{14,12},{16,18},{18,... | collective-permute-start | bytes 8847368 | tf_op jit(solution)/shard_map/ppermute | solution.py:226
  1.4 0.7 copy-start.1
  2.1 0.7 copy-start.2
  6.1 2.4 %collective-permute-start.1 = (bf16[768,512]{1,0:T(8,128)(2,1)S(1)}, bf16[768,512]{1,0:T(8,128)(2,1)S(1)}, u32[]{:S(2)}, u32[]{:S(2)}) collective-permute-start(bf16[768,512]{1,0:T(8,128)(2,1)S(1)} %get-tuple-element.31.rest_0_.rest_2_), channel_id=1, source_target_pairs={{0,2},{2,0},{4,6},{6,4},{8,10},{10,8},{12,14},{14,12},{16,18},{18,... | collective-permute-start | bytes 2359304 | tf_op jit(solution)/shard_map/ppermute | solution.py:226
  6.2 3.4 %collective-permute-start.2 = (bf16[768,512]{1,0:T(8,128)(2,1)S(1)}, bf16[768,512]{1,0:T(8,128)(2,1)S(1)}, u32[]{:S(2)}, u32[]{:S(2)}) collective-permute-start(bf16[768,512]{1,0:T(8,128)(2,1)S(1)} %get-tuple-element.33.rest_0_), channel_id=1, source_target_pairs={{0,2},{2,0},{4,6},{6,4},{8,10},{10,8},{12,14},{14,12},{16,18},{18,... | collective-permute-start | bytes 2359304 | tf_op jit(solution)/shard_map/ppermute | solution.py:226
  11.6 33.6 %collective-permute-start.17 = (bf16[2,2,40,768]{3,2,1,0:T(8,128)(2,1)S(1)}, bf16[2,2,40,768]{3,2,1,0:T(8,128)(2,1)S(1)}, u32[]{:S(2)}, u32[]{:S(2)}) collective-permute-start(bf16[2,2,40,768]{3,2,1,0:T(8,128)(2,1)S(1)} %get-tuple-element.50), channel_id=1, source_target_pairs={{0,8},{2,10},{4,12},{6,14},{8,0},{10,2},{12,4},{14,6},{16,24},{18,... | collective-permute-start | bytes 737288 | tf_op jit(solution)/shard_map/ppermute | solution.py:226
  14.3 13.1 %collective-permute-start.18 = (bf16[2,2,40,768]{3,2,1,0:T(8,128)(2,1)S(1)}, bf16[2,2,40,768]{3,2,1,0:T(8,128)(2,1)S(1)}, u32[]{:S(2)}, u32[]{:S(2)}) collective-permute-start(bf16[2,2,40,768]{3,2,1,0:T(8,128)(2,1)S(1)} %get-tuple-element.52), channel_id=1, source_target_pairs={{0,8},{2,10},{4,12},{6,14},{8,0},{10,2},{12,4},{14,6},{16,24},{18,... | collective-permute-start | bytes 737288 | tf_op jit(solution)/shard_map/ppermute | solution.py:226
  15.9 31.6 %collective-permute-start.10 = (bf16[2,2,64,768]{3,2,1,0:T(8,128)(2,1)S(1)}, bf16[2,2,64,768]{3,2,1,0:T(8,128)(2,1)S(1)}, u32[]{:S(2)}, u32[]{:S(2)}) collective-permute-start(bf16[2,2,64,768]{3,2,1,0:T(8,128)(2,1)S(1)} %get-tuple-element.42), channel_id=1, source_target_pairs={{0,1},{1,0},{2,3},{3,2},{4,5},{5,4},{6,7},{7,6},{8,9},{9,8},{10,11... | collective-permute-start | bytes 1179656 | tf_op jit(solution)/shard_map/ppermute | solution.py:224
  17.8 17.7 %collective-permute-start.11 = (bf16[2,2,64,768]{3,2,1,0:T(8,128)(2,1)S(1)}, bf16[2,2,64,768]{3,2,1,0:T(8,128)(2,1)S(1)}, u32[]{:S(2)}, u32[]{:S(2)}) collective-permute-start(bf16[2,2,64,768]{3,2,1,0:T(8,128)(2,1)S(1)} %get-tuple-element.44), channel_id=1, source_target_pairs={{0,1},{1,0},{2,3},{3,2},{4,5},{5,4},{6,7},{7,6},{8,9},{9,8},{10,11... | collective-permute-start | bytes 1179656 | tf_op jit(solution)/shard_map/ppermute | solution.py:224
  20.3 32.5 %collective-permute-start.3 = (bf16[2,2,80,768]{3,2,1,0:T(8,128)(2,1)S(1)}, bf16[2,2,80,768]{3,2,1,0:T(8,128)(2,1)S(1)}, u32[]{:S(2)}, u32[]{:S(2)}) collective-permute-start(bf16[2,2,80,768]{3,2,1,0:T(8,128)(2,1)S(1)} %get-tuple-element.34), channel_id=1, source_target_pairs={{0,4},{2,6},{4,0},{6,2},{8,12},{10,14},{12,8},{14,10},{16,20},{18,... | collective-permute-start | bytes 1474568 | tf_op jit(solution)/shard_map/ppermute | solution.py:226
  27.4 16.2 %collective-permute-start.4 = (bf16[2,2,80,768]{3,2,1,0:T(8,128)(2,1)S(1)}, bf16[2,2,80,768]{3,2,1,0:T(8,128)(2,1)S(1)}, u32[]{:S(2)}, u32[]{:S(2)}) collective-permute-start(bf16[2,2,80,768]{3,2,1,0:T(8,128)(2,1)S(1)} %get-tuple-element.36), channel_id=1, source_target_pairs={{0,4},{2,6},{4,0},{6,2},{8,12},{10,14},{12,8},{14,10},{16,20},{18,... | collective-permute-start | bytes 1474568 | tf_op jit(solution)/shard_map/ppermute | solution.py:226
  35.5 11.4 %collective-permute-start.20 = (bf16[2,40,768]{2,1,0:T(8,128)(2,1)S(1)}, bf16[2,40,768]{2,1,0:T(8,128)(2,1)S(1)}, u32[]{:S(2)}, u32[]{:S(2)}) collective-permute-start(bf16[2,40,768]{2,1,0:T(8,128)(2,1)S(1)} %get-tuple-element.67), channel_id=1, source_target_pairs={{0,1},{1,0},{2,3},{3,2},{4,5},{5,4},{6,7},{7,6},{8,9},{9,8},{10,11... | collective-permute-start | bytes 368648 | tf_op jit(solution)/shard_map/ppermute | solution.py:224
  43.5 28.5 %collective-permute-start.19 = (bf16[2,40,768]{2,1,0:T(8,128)(2,1)S(1)}, bf16[2,40,768]{2,1,0:T(8,128)(2,1)S(1)}, u32[]{:S(2)}, u32[]{:S(2)}) collective-permute-start(bf16[2,40,768]{2,1,0:T(8,128)(2,1)S(1)} %get-tuple-element.68), channel_id=1, source_target_pairs={{0,1},{1,0},{2,3},{3,2},{4,5},{5,4},{6,7},{7,6},{8,9},{9,8},{10,11... | collective-permute-start | bytes 368648 | tf_op jit(solution)/shard_map/ppermute | solution.py:224
  45.2 5.9 %collective-permute-start.13 = (bf16[2,64,768]{2,1,0:T(8,128)(2,1)S(1)}, bf16[2,64,768]{2,1,0:T(8,128)(2,1)S(1)}, u32[]{:S(2)}, u32[]{:S(2)}) collective-permute-start(bf16[2,64,768]{2,1,0:T(8,128)(2,1)S(1)} %get-tuple-element.63), channel_id=1, source_target_pairs={{0,8},{2,10},{4,12},{6,14},{8,0},{10,2},{12,4},{14,6},{16,24},{18,... | collective-permute-start | bytes 589832 | tf_op jit(solution)/shard_map/ppermute | solution.py:226
  46.9 8.2 %collective-permute-start.6 = (bf16[2,80,768]{2,1,0:T(8,128)(2,1)S(1)}, bf16[2,80,768]{2,1,0:T(8,128)(2,1)S(1)}, u32[]{:S(2)}, u32[]{:S(2)}) collective-permute-start(bf16[2,80,768]{2,1,0:T(8,128)(2,1)S(1)} %get-tuple-element.61), channel_id=1, source_target_pairs={{0,1},{1,0},{2,3},{3,2},{4,5},{5,4},{6,7},{7,6},{8,9},{9,8},{10,11... | collective-permute-start | bytes 737288 | tf_op jit(solution)/shard_map/ppermute | solution.py:224
  47.5 24.6 %collective-permute-start.22 = (bf16[40,768]{1,0:T(8,128)(2,1)S(1)}, bf16[40,768]{1,0:T(8,128)(2,1)S(1)}, u32[]{:S(2)}, u32[]{:S(2)}) collective-permute-start(bf16[40,768]{1,0:T(8,128)(2,1)S(1)} %get-tuple-element.65), channel_id=1, source_target_pairs={{0,4},{2,6},{4,0},{6,2},{8,12},{10,14},{12,8},{14,10},{16,20},{18,... | collective-permute-start | bytes 184328 | tf_op jit(solution)/shard_map/ppermute | solution.py:226
  51.1 6.9 %collective-permute-start.12 = (bf16[2,64,768]{2,1,0:T(8,128)(2,1)S(1)}, bf16[2,64,768]{2,1,0:T(8,128)(2,1)S(1)}, u32[]{:S(2)}, u32[]{:S(2)}) collective-permute-start(bf16[2,64,768]{2,1,0:T(8,128)(2,1)S(1)} %get-tuple-element.64), channel_id=1, source_target_pairs={{0,8},{2,10},{4,12},{6,14},{8,0},{10,2},{12,4},{14,6},{16,24},{18,... | collective-permute-start | bytes 589832 | tf_op jit(solution)/shard_map/ppermute | solution.py:226
  52.8 9.7 %collective-permute-start.5 = (bf16[2,80,768]{2,1,0:T(8,128)(2,1)S(1)}, bf16[2,80,768]{2,1,0:T(8,128)(2,1)S(1)}, u32[]{:S(2)}, u32[]{:S(2)}) collective-permute-start(bf16[2,80,768]{2,1,0:T(8,128)(2,1)S(1)} %get-tuple-element.62), channel_id=1, source_target_pairs={{0,1},{1,0},{2,3},{3,2},{4,5},{5,4},{6,7},{7,6},{8,9},{9,8},{10,11... | collective-permute-start | bytes 737288 | tf_op jit(solution)/shard_map/ppermute | solution.py:224
  55.1 7.3 %collective-permute-start.15 = (bf16[64,768]{1,0:T(8,128)(2,1)S(1)}, bf16[64,768]{1,0:T(8,128)(2,1)S(1)}, u32[]{:S(2)}, u32[]{:S(2)}) collective-permute-start(bf16[64,768]{1,0:T(8,128)(2,1)S(1)} %get-tuple-element.59), channel_id=1, source_target_pairs={{0,16},{2,18},{4,20},{6,22},{8,24},{10,26},{12,28},{14,30},{16,0},... | collective-permute-start | bytes 294920 | tf_op jit(solution)/shard_map/ppermute | solution.py:226
  58.0 16.1 %collective-permute-start.21 = (bf16[40,768]{1,0:T(8,128)(2,1)S(1)}, bf16[40,768]{1,0:T(8,128)(2,1)S(1)}, u32[]{:S(2)}, u32[]{:S(2)}) collective-permute-start(bf16[40,768]{1,0:T(8,128)(2,1)S(1)} %get-tuple-element.66), channel_id=1, source_target_pairs={{0,4},{2,6},{4,0},{6,2},{8,12},{10,14},{12,8},{14,10},{16,20},{18,... | collective-permute-start | bytes 184328 | tf_op jit(solution)/shard_map/ppermute | solution.py:226
  62.4 5.2 %collective-permute-start.8 = (bf16[80,768]{1,0:T(8,128)(2,1)S(1)}, bf16[80,768]{1,0:T(8,128)(2,1)S(1)}, u32[]{:S(2)}, u32[]{:S(2)}) collective-permute-start(bf16[80,768]{1,0:T(8,128)(2,1)S(1)} %get-tuple-element.57), channel_id=1, source_target_pairs={{0,8},{2,10},{4,12},{6,14},{8,0},{10,2},{12,4},{14,6},{16,24},{18,... | collective-permute-start | bytes 368648 | tf_op jit(solution)/shard_map/ppermute | solution.py:226
  62.5 18.2 %collective-permute-start.14 = (bf16[64,768]{1,0:T(8,128)(2,1)S(1)}, bf16[64,768]{1,0:T(8,128)(2,1)S(1)}, u32[]{:S(2)}, u32[]{:S(2)}) collective-permute-start(bf16[64,768]{1,0:T(8,128)(2,1)S(1)} %get-tuple-element.60), channel_id=1, source_target_pairs={{0,16},{2,18},{4,20},{6,22},{8,24},{10,26},{12,28},{14,30},{16,0},... | collective-permute-start | bytes 294920 | tf_op jit(solution)/shard_map/ppermute | solution.py:226
  67.6 13.0 %collective-permute-start.16 = (bf16[64,768]{1,0:T(8,128)(2,1)S(1)}, bf16[64,768]{1,0:T(8,128)(2,1)S(1)}, u32[]{:S(2)}, u32[]{:S(2)}) collective-permute-start(bf16[64,768]{1,0:T(8,128)(2,1)S(1)} %fusion.12), channel_id=1, source_target_pairs={{0,4},{2,6},{4,0},{6,2},{8,12},{10,14},{12,8},{14,10},{16,20},{18,... | collective-permute-start | bytes 294920 | tf_op jit(solution)/shard_map/ppermute | solution.py:226
  72.0 8.6 %collective-permute-start.7 = (bf16[80,768]{1,0:T(8,128)(2,1)S(1)}, bf16[80,768]{1,0:T(8,128)(2,1)S(1)}, u32[]{:S(2)}, u32[]{:S(2)}) collective-permute-start(bf16[80,768]{1,0:T(8,128)(2,1)S(1)} %get-tuple-element.58), channel_id=1, source_target_pairs={{0,8},{2,10},{4,12},{6,14},{8,0},{10,2},{12,4},{14,6},{16,24},{18,... | collective-permute-start | bytes 368648 | tf_op jit(solution)/shard_map/ppermute | solution.py:226
  72.1 8.6 %collective-permute-start.9 = (bf16[80,768]{1,0:T(8,128)(2,1)S(1)}, bf16[80,768]{1,0:T(8,128)(2,1)S(1)}, u32[]{:S(2)}, u32[]{:S(2)}) collective-permute-start(bf16[80,768]{1,0:T(8,128)(2,1)S(1)} %fusion.8), channel_id=1, source_target_pairs={{0,16},{2,18},{4,20},{6,22},{8,24},{10,26},{12,28},{14,30},{16,0},... | collective-permute-start | bytes 368648 | tf_op jit(solution)/shard_map/ppermute | solution.py:226
  74.1 6.5 %collective-permute-start.23 = (bf16[40,768]{1,0:T(8,128)(2,1)S(1)}, bf16[40,768]{1,0:T(8,128)(2,1)S(1)}, u32[]{:S(2)}, u32[]{:S(2)}) collective-permute-start(bf16[40,768]{1,0:T(8,128)(2,1)S(1)} %fusion.16), channel_id=1, source_target_pairs={{0,16},{2,18},{4,20},{6,22},{8,24},{10,26},{12,28},{14,30},{16,0},... | collective-permute-start | bytes 184328 | tf_op jit(solution)/shard_map/ppermute | solution.py:226
